TPU v7x, 32 devices: a whole 2x2x4 slice. The times are simulated.
32 devices in a mesh: depth: 4 (over y, core), blk: 8 (over z, x).
Axes of the slice: x: 2, y: 2, z: 4, core: 2. Of those that a mesh axis runs over, the one named last changes fastest.
Arguments:
- jacobian: bfloat16 [96, 16384], P(('depth', 'blk')), may hold values from -6 to 6
- gain_inverse: bfloat16 [16384, 16384], P('depth', 'blk'), may hold values from -0.00024414062 to 0.00048828125, as said below
- variance: float32 [96], P(('depth', 'blk')), may hold values from 2 to 12
Outputs:
- omega_diag: float32 [96], P(('depth', 'blk'))
Inputs may be any that keep to these rules, and one draw needn't show every extreme that they name: gain_inverse is symmetric and positive definite.
All inputs are finite; a program needn't handle non-finite values.
Results may differ from a plain program's by a relative error of at most 0.0003.
Values may be sent and summed in bfloat16 or wider, within the bound.
A program may use at most 128 MiB of HBM per device.

v0:
```python
import functools

import jax
import jax.numpy as jnp
from jax import lax
from jax.experimental import pallas as pl
from jax.experimental.pallas import tpu as pltpu
from jax.sharding import PartitionSpec as P

LANES = 128
SUBLANES = 8
MESH = pl.DeviceIdType.MESH


def exchange_kernel(depth_count, blk_count, slots, *refs):
    count = len(slots)
    sources, targets = refs[:count], refs[count : 2 * count]
    send_sem, recv_sem, own_sem = refs[2 * count :]
    devices = depth_count * blk_count
    me = lax.axis_index("depth") * blk_count + lax.axis_index("blk")

    def place(device):
        return {"depth": device // blk_count, "blk": lax.rem(device, blk_count)}

    def peer(step):
        return lax.rem(me + step, devices)

    def slot_of(kind, device):
        if kind == "depth":
            return device // blk_count
        if kind == "blk":
            return lax.rem(device, blk_count)
        return device

    def copy(which, step):
        device = peer(step)
        return pltpu.make_async_remote_copy(
            src_ref=sources[which].at[slot_of(slots[which], device)],
            dst_ref=targets[which].at[me],
            send_sem=send_sem.at[which, step],
            recv_sem=recv_sem.at[which, step],
            device_id=place(device),
            device_id_type=MESH,
        )

    barrier = pltpu.get_barrier_semaphore()

    @pl.loop(1, devices)
    def _(step):
        pl.semaphore_signal(barrier, inc=1, device_id=place(peer(step)), device_id_type=MESH)

    own = [
        pltpu.make_async_copy(sources[w].at[slot_of(slots[w], me)], targets[w].at[me], own_sem.at[w])
        for w in range(count)
    ]
    for w in range(count):
        own[w].start()
    pl.semaphore_wait(barrier, devices - 1)

    @pl.loop(1, devices)
    def _(step):
        for w in range(count):
            copy(w, step).start()

    for w in range(count):
        own[w].wait()

    @pl.loop(1, devices)
    def _(step):
        for w in range(count):
            copy(w, step).wait()


def exchange(slots, collective_id, *operands):
    depth_count = lax.axis_size("depth")
    blk_count = lax.axis_size("blk")
    devices = depth_count * blk_count
    count = len(slots)
    vmem = pl.BlockSpec(memory_space=pltpu.VMEM)
    return pl.pallas_call(
        functools.partial(exchange_kernel, depth_count, blk_count, slots),
        out_shape=[jax.ShapeDtypeStruct((devices,) + x.shape[1:], x.dtype) for x in operands],
        in_specs=[vmem] * count,
        out_specs=[vmem] * count,
        scratch_shapes=[
            pltpu.SemaphoreType.DMA((count, devices)),
            pltpu.SemaphoreType.DMA((count, devices)),
            pltpu.SemaphoreType.DMA((count,)),
        ],
        compiler_params=pltpu.CompilerParams(collective_id=collective_id, has_side_effects=True),
    )(*operands)


def sections(jacobian, parts):
    rows, states = jacobian.shape
    width = states // parts
    return jacobian.reshape(rows, parts, width // LANES, LANES).transpose(1, 0, 2, 3)


def shards(jacobian, gain_inverse, variance):
    rows = jacobian.shape[0]
    depth_count = lax.axis_size("depth")
    blk_count = lax.axis_size("blk")
    devices = depth_count * blk_count
    left, right = exchange(
        ("depth", "blk"), 0, sections(jacobian, depth_count), sections(jacobian, blk_count)
    )
    left = left.reshape(devices * rows, -1)
    panel = right.reshape(devices * rows, -1)
    projected = jnp.dot(left, gain_inverse, preferred_element_type=jnp.float32)
    partial_sum = jnp.sum(projected * panel.astype(jnp.float32), axis=1)
    padded = jnp.pad(
        partial_sum.reshape(devices, 1, rows), ((0, 0), (0, SUBLANES - 1), (0, LANES - rows))
    )
    (gathered,) = exchange(("all",), 1, padded)
    quadratic = jnp.sum(gathered[:, 0, :rows], axis=0)
    return variance - quadratic


def solution(mesh):
    in_specs = (P(("depth", "blk"), None), P("depth", "blk"), P(("depth", "blk")))
    out_specs = P(("depth", "blk"))
    return jax.shard_map(shards, mesh=mesh, in_specs=in_specs, out_specs=out_specs, check_vma=False)
```

profile of v0, /device:TPU:0, one launch (start us, length us, event | category | flops | bytes accessed | tf_op | source)
XLA Modules:
  0.0 61.5 jit_solution(2897210296628969804)
XLA Ops:
  0.0 0.0 copy-start
  0.0 0.9 %copy.8 = bf16[1,3,128,128]{3,2,1,0:T(8,128)(2,1)S(1)} copy(bf16[1,3,128,128]{3,1,2,0:T(4,128)(2,1)} %bitcast.30) | data formatting | bytes 196608
  0.9 0.6 %copy.19 = bf16[3,8,16,128]{3,2,0,1:T(8,128)(2,1)} copy(bf16[3,8,16,128]{3,2,1,0:T(8,128)(2,1)S(1)} %bitcast.25) | data formatting | bytes 196608 | tf_op jit(solution)/shard_map/reshape | solution.py:97
  1.6 0.6 %copy.20 = bf16[3,4,32,128]{3,2,0,1:T(8,128)(2,1)} copy(bf16[3,4,32,128]{3,2,1,0:T(8,128)(2,1)S(1)} %bitcast.26) | data formatting | bytes 196608 | tf_op jit(solution)/shard_map/reshape | solution.py:97
  2.2 34.9 %shard_map.37 = (bf16[32,3,32,128]{3,2,1,0:T(8,128)(2,1)}, bf16[32,3,16,128]{3,2,1,0:T(8,128)(2,1)}) custom-call(bf16[4,3,32,128]{3,2,1,0:T(8,128)(2,1)} %bitcast.28, bf16[8,3,16,128]{3,2,1,0:T(8,128)(2,1)} %bitcast.27), custom_call_target="tpu_custom_call" | custom-call | tf_op jit(solution)/shard_map/pallas_call | solution.py:80
  37.1 1.1 %convert.1 = f32[12,8,16,128]{3,2,1,0:T(8,128)S(1)} convert(bf16[12,8,16,128]{3,2,1,0:T(8,128)(2,1)} %bitcast.29) | non-fusion elementwise | flops 196608 | bytes 1179648
  38.2 9.1 %fusion = f32[96]{0:T(128)S(1)} fusion(bf16[4096,2048]{1,0:T(8,128)(2,1)} %param.4, f32[12,8,16,128]{3,2,1,0:T(8,128)S(1)} %convert.1, bf16[12,8,32,128]{3,2,1,0:T(8,128)(2,1)} %bitcast.24), kind=kOutput, calls=%fused_computation.1 | convolution fusion | flops 1611005824 | bytes 18350464 | tf_op jit(solution)/shard_map/dot_general | solution.py:110
  47.3 0.1 reshape.18
  47.4 0.7 %pad.4.refs_0_ = f32[32,8,128]{2,1,0:T(8,128)} pad(f32[32,1,3]{2,1,0:T(1,128)S(1)} %bitcast.31, f32[]{:T(128)} %constant.1.clone.1), padding=0_0x0_7x0_125 | pad | bytes 131460 | tf_op jit(solution)/shard_map/jit(_pad)/pad | solution.py:112
  48.0 12.0 %shard_map.38 = f32[32,8,128]{2,1,0:T(8,128)} custom-call(f32[32,8,128]{2,1,0:T(8,128)} %pad.4.refs_0_), custom_call_target="tpu_custom_call" | custom-call | tf_op jit(solution)/shard_map/pallas_call | solution.py:80
  60.0 1.0 %slice_reduce_fusion = f32[3]{0:T(128)S(1)} fusion(f32[32,8,128]{2,1,0:T(8,128)} %shard_map.38), kind=kLoop, calls=%fused_computation.6 | loop fusion | flops 93 | bytes 396 | tf_op jit(solution)/shard_map/reduce_sum | solution.py:116
  61.0 0.0 copy-done
  61.0 0.5 sub.3
Async XLA Ops:
  0.0 61.0 %copy-start = (f32[3]{0:T(128)S(1)}, f32[3]{0:T(128)}, u32[]{:S(2)}) copy-start(f32[3]{0:T(128)} %param.5) | copy-start | bytes 40
where the time goes:
time: 61.8 us; the launch traced here: 61.5 us
  Pallas kernels  46.9 us (76%)
  matrix products  9.1 us (15%)
  local copies, waits for them, and re-layouts  2.98 us (5%)
  other arithmetic  2.53 us (4%)
    pallas_call x2, Pallas kernels, exchange(): pl.pallas_call(functools.partial(exchange_kernel, depth_count, blk_count,...  46.9 us
    dot_general x1, matrix products, shards(): projected = jnp.dot(left, gain_inverse, preferred_element_type=jnp.float32)  9.1 us
    reshape x2, local copies, waits for them, and re-layouts, sections(): jacobian.reshape(rows, parts, width // LANES, LANES).transpose(1, 0, 2, 3)  1.28 us

commit v1 on v0

--- a/solution.py
+++ b/solution.py
@@ -9,6 +9,7 @@
 
 LANES = 128
 SUBLANES = 8
+PACKED = 16
 MESH = pl.DeviceIdType.MESH
 
 
@@ -97,7 +98,7 @@
     return jacobian.reshape(rows, parts, width // LANES, LANES).transpose(1, 0, 2, 3)
 
 
-def shards(jacobian, gain_inverse, variance):
+def plain_shards(jacobian, gain_inverse, variance):
     rows = jacobian.shape[0]
     depth_count = lax.axis_size("depth")
     blk_count = lax.axis_size("blk")
@@ -117,7 +118,339 @@
     return variance - quadratic
 
 
+def half_kernel(
+    depth_count, blk_count, rows, jac_ref, gain_ref, out_ref,
+    own_raw, own_wide, lines, other_in, panel_in, other_out, panel_out, wide,
+    gain, left, parts, arrived,
+    local_sem, chain_send, chain_recv, plane_send, plane_recv, last_send, last_recv,
+):
+    per = blk_count // depth_count
+    planes = depth_count
+    group = depth_count * per
+    devices = depth_count * blk_count
+    states = jac_ref.shape[1]
+    chunks = states // LANES
+    sub = states // blk_count // LANES
+    width = sub * LANES
+    pitch = rows * sub + 1
+    depth = lax.axis_index("depth")
+    blk = lax.axis_index("blk")
+    plane = blk // per
+    side = lax.rem(blk, per)
+    spot = depth * per + side
+    on_diagonal = plane == depth
+
+    def other_half(d, z, s):
+        return jnp.where(d < z, s, per - 1 - s)
+
+    def other_section(d, z, s):
+        return d * per + other_half(d, z, s)
+
+    def peer(step):
+        return lax.rem(spot + step, group)
+
+    def place(member, z):
+        return {"depth": member // per, "blk": z * per + lax.rem(member, per)}
+
+    half = other_half(depth, plane, side)
+    jac_copy = pltpu.make_async_copy(jac_ref, own_raw, local_sem.at[0])
+    jac_copy.start()
+    gain_other = pltpu.make_async_copy(
+        gain_ref.at[pl.ds(pl.multiple_of(half * width, width), width), :], gain.at[0], local_sem.at[1]
+    )
+    gain_own = pltpu.make_async_copy(
+        gain_ref.at[pl.ds(pl.multiple_of(side * width, width), width), :], gain.at[1], local_sem.at[2]
+    )
+    gain_other.start()
+
+    @pl.when(on_diagonal)
+    def _():
+        gain_own.start()
+
+    barrier = pltpu.get_barrier_semaphore()
+
+    @pl.loop(1, devices)
+    def _(step):
+        target = lax.rem(depth * blk_count + blk + step, devices)
+        pl.semaphore_signal(
+            barrier, inc=1,
+            device_id={"depth": target // blk_count, "blk": lax.rem(target, blk_count)},
+            device_id_type=MESH,
+        )
+
+    jac_copy.wait()
+    for c in range(chunks):
+        own_wide[pl.ds(c, rows, stride=chunks), :] = own_raw[:, c * LANES : (c + 1) * LANES].astype(
+            jnp.float32
+        )
+    for r in range(rows):
+        lines[plane, r] = own_wide[r * chunks : (r + 1) * chunks, :].astype(jnp.bfloat16)
+
+    pl.semaphore_wait(barrier, devices - 1)
+
+    def chain(source, target, way):
+        return pltpu.make_async_remote_copy(
+            src_ref=lines.at[source],
+            dst_ref=lines.at[source],
+            send_sem=chain_send.at[source, way],
+            recv_sem=chain_recv.at[source],
+            device_id={"depth": depth, "blk": target * per + side},
+            device_id_type=MESH,
+        )
+
+    def section_of(source, section):
+        return lines.at[source, :, pl.ds(pl.multiple_of(section * sub, sub), sub), :]
+
+    def to_other(source, step):
+        member = peer(step)
+        section = other_section(member // per, plane, lax.rem(member, per))
+        return pltpu.make_async_remote_copy(
+            src_ref=section_of(source, section),
+            dst_ref=other_in.at[source, spot],
+            send_sem=plane_send.at[0, source, step],
+            recv_sem=plane_recv.at[0, source, spot],
+            device_id=place(member, plane),
+            device_id_type=MESH,
+        )
+
+    def to_panel(source, step):
+        member = peer(step)
+        return pltpu.make_async_remote_copy(
+            src_ref=section_of(source, plane * per + lax.rem(member, per)),
+            dst_ref=panel_in.at[source, spot],
+            send_sem=plane_send.at[1, source, step],
+            recv_sem=plane_recv.at[1, source, spot],
+            device_id=place(member, plane),
+            device_id_type=MESH,
+        )
+
+    def spread(source):
+        @pl.loop(1, group)
+        def _(step):
+            to_other(source, step).start()
+            to_panel(source, step).start()
+
+    def stages(act):
+        for distance in range(1, planes):
+            below = plane - distance
+            above = plane + distance
+
+            @pl.when(below >= 0)
+            def _():
+                act(below, plane + 1, 0)
+
+            @pl.when(above < planes)
+            def _():
+                act(above, plane - 1, 1)
+
+    @pl.when(plane + 1 < planes)
+    def _():
+        chain(plane, plane + 1, 0).start()
+
+    @pl.when(plane > 0)
+    def _():
+        chain(plane, plane - 1, 1).start()
+
+    spread(plane)
+
+    def pass_on(source, onward, way):
+        chain(source, source, way).wait_recv()
+
+        @pl.when((onward < planes) & (onward >= 0))
+        def _():
+            chain(source, onward, way).start()
+
+        spread(source)
+
+    stages(pass_on)
+
+    my_other = other_section(depth, plane, side)
+
+    def widen(index, slot, block):
+        wide[index, pl.ds(slot * pitch, rows * sub), :] = block.reshape(rows * sub, LANES).astype(
+            jnp.float32
+        )
+
+    def slot_of(source, member):
+        return (member // per) * blk_count + source * per + lax.rem(member, per)
+
+    def collect(source):
+        widen(0, slot_of(source, spot), section_of(source, my_other)[...])
+        widen(1, slot_of(source, spot), section_of(source, blk)[...])
+
+        @pl.loop(1, group)
+        def _(step):
+            member = peer(step)
+            slot = slot_of(source, member)
+            for which, buffer in enumerate((other_in, panel_in)):
+                pltpu.make_async_copy(
+                    buffer.at[source, member], buffer.at[source, member], plane_recv.at[which, source, member]
+                ).wait()
+                widen(which, slot, buffer[source, member])
+
+    collect(plane)
+    stages(lambda source, onward, way: collect(source))
+
+    def columns(index, c):
+        return [
+            wide[index, pl.ds(r * sub + c, devices, stride=pitch), :] for r in range(rows)
+        ]
+
+    for c in range(sub):
+        for r, block in enumerate(columns(0, c)):
+            left[0, r * devices : (r + 1) * devices, c * LANES : (c + 1) * LANES] = block.astype(
+                jnp.bfloat16
+            )
+
+    block_width = 4 * LANES
+
+    def quadratic(index):
+        total = [jnp.zeros((devices, LANES), jnp.float32) for _ in range(rows)]
+        for n in range(width // block_width):
+            product = jnp.dot(
+                left[index], gain[index, :, n * block_width : (n + 1) * block_width],
+                preferred_element_type=jnp.float32,
+            )
+            for c in range(block_width // LANES):
+                panel = columns(1, n * (block_width // LANES) + c)
+                for r in range(rows):
+                    total[r] += (
+                        product[r * devices : (r + 1) * devices, c * LANES : (c + 1) * LANES] * panel[r]
+                    )
+        return total
+
+    gain_other.wait()
+    weight = jnp.where(on_diagonal, 1.0, 2.0)
+    for r, part in enumerate(quadratic(0)):
+        parts[r] = part * weight
+
+    @pl.when(on_diagonal)
+    def _():
+        for c in range(sub):
+            for r, block in enumerate(columns(1, c)):
+                left[1, r * devices : (r + 1) * devices, c * LANES : (c + 1) * LANES] = block.astype(
+                    jnp.bfloat16
+                )
+        gain_own.wait()
+        for r, part in enumerate(quadratic(1)):
+            parts[r] += part
+
+    lane = lax.broadcasted_iota(jnp.int32, (devices, LANES), 1)
+    packed = jnp.zeros((devices, LANES), jnp.float32)
+    for r in range(rows):
+        packed = jnp.where(lane == r, jnp.sum(parts[r], axis=1, keepdims=True), packed)
+    for t in range(devices):
+        arrived[devices + t] = packed[t : t + 1]
+
+    me = depth * blk_count + blk
+
+    def last(step):
+        target = lax.rem(me + step, devices)
+        return pltpu.make_async_remote_copy(
+            src_ref=arrived.at[devices + target],
+            dst_ref=arrived.at[me],
+            send_sem=last_send.at[step],
+            recv_sem=last_recv.at[step],
+            device_id={"depth": target // blk_count, "blk": lax.rem(target, blk_count)},
+            device_id_type=MESH,
+        )
+
+    @pl.loop(1, devices)
+    def _(step):
+        last(step).start()
+
+    arrived[me] = arrived[devices + me]
+
+    def sent(source, onward, way):
+        @pl.when((onward < planes) & (onward >= 0))
+        def _():
+            chain(source, onward, way).wait_send()
+
+        @pl.loop(1, group)
+        def _(step):
+            to_other(source, step).wait_send()
+            to_panel(source, step).wait_send()
+
+    @pl.when(plane + 1 < planes)
+    def _():
+        chain(plane, plane + 1, 0).wait_send()
+
+    @pl.when(plane > 0)
+    def _():
+        chain(plane, plane - 1, 1).wait_send()
+
+    @pl.loop(1, group)
+    def _(step):
+        to_other(plane, step).wait_send()
+        to_panel(plane, step).wait_send()
+
+    stages(sent)
+
+    @pl.loop(1, devices)
+    def _(step):
+        last(step).wait()
+
+    total = arrived[0]
+    for t in range(1, devices):
+        total += arrived[t]
+    out_ref[...] = total
+
+
+def half_shards(jacobian, gain_inverse, variance):
+    rows, states = jacobian.shape
+    depth_count = lax.axis_size("depth")
+    blk_count = lax.axis_size("blk")
+    devices = depth_count * blk_count
+    per = blk_count // depth_count
+    planes, group = depth_count, depth_count * per
+    chunks = states // LANES
+    sub = states // blk_count // LANES
+    width = sub * LANES
+    bf16, f32 = jnp.bfloat16, jnp.float32
+    dma = pltpu.SemaphoreType.DMA
+    quadratic = pl.pallas_call(
+        functools.partial(half_kernel, depth_count, blk_count, rows),
+        out_shape=jax.ShapeDtypeStruct((1, LANES), f32),
+        in_specs=[pl.BlockSpec(memory_space=pl.ANY)] * 2,
+        out_specs=pl.BlockSpec(memory_space=pltpu.VMEM),
+        scratch_shapes=[
+            pltpu.VMEM((rows, states), bf16),
+            pltpu.VMEM((rows * chunks, LANES), f32),
+            pltpu.VMEM((planes, rows, chunks, LANES), bf16),
+            pltpu.VMEM((planes, group, rows, sub, LANES), bf16),
+            pltpu.VMEM((planes, group, rows, sub, LANES), bf16),
+            pltpu.VMEM((SUBLANES, LANES), bf16),
+            pltpu.VMEM((SUBLANES, LANES), bf16),
+            pltpu.VMEM((2, devices * (rows * sub + 1), LANES), f32),
+            pltpu.VMEM((2, width, width), bf16),
+            pltpu.VMEM((2, rows * devices, width), bf16),
+            pltpu.VMEM((rows, devices, LANES), f32),
+            pltpu.VMEM((2 * devices, 1, LANES), f32),
+            dma((3,)),
+            dma((planes, 2)),
+            dma((planes,)),
+            dma((2, planes, group)),
+            dma((2, planes, group)),
+            dma((devices,)),
+            dma((devices,)),
+        ],
+        compiler_params=pltpu.CompilerParams(
+            collective_id=0, has_side_effects=True, vmem_limit_bytes=60 * 1024 * 1024
+        ),
+    )(jacobian, gain_inverse)
+    return variance - quadratic[0, :rows]
+
+
 def solution(mesh):
     in_specs = (P(("depth", "blk"), None), P("depth", "blk"), P(("depth", "blk")))
     out_specs = P(("depth", "blk"))
+    depth_count, blk_count = mesh.shape["depth"], mesh.shape["blk"]
+
+    def shards(jacobian, gain_inverse, variance):
+        width = gain_inverse.shape[1]
+        fits = gain_inverse.size * gain_inverse.dtype.itemsize <= 16 * 1024 * 1024
+        if blk_count == 2 * depth_count and width % (PACKED * LANES) == 0 and fits:
+            return half_shards(jacobian, gain_inverse, variance)
+        return plain_shards(jacobian, gain_inverse, variance)
+
     return jax.shard_map(shards, mesh=mesh, in_specs=in_specs, out_specs=out_specs, check_vma=False)

time: 61.8 us -> 33.6 us (0.54)
  Pallas kernels: 46.9 us -> 32.3 us
  matrix products: 9.1 us -> 0 us
  local copies, waits for them, and re-layouts: 2.98 us -> 0.01 us
  other arithmetic: 2.53 us -> 1.11 us
    pallas_call x2 -> x1, Pallas kernels: 46.9 us -> 32.3 us  [half_shards(): pl.pallas_call(functools.partial(half_kernel, depth_count, blk_count, row...]
    dot_general x1 -> x0, matrix products: 9.1 us -> none  [shards(): projected = jnp.dot(left, gain_inverse, preferred_element_type=jnp.float32)]
    reshape x3 -> x0, local copies, waits for them, and re-layouts: 1.38 us -> none  [the longest x2 1.28 us: sections(): jacobian.reshape(rows, parts, width // LANES, LANES).transpose(1, 0, 2, 3)]
    unnamed x1 -> x0, other arithmetic: 1.06 us -> none
    reduce_sum x1 -> x0, other arithmetic: 0.96 us -> none  [shards(): quadratic = jnp.sum(gathered[:, 0, :rows], axis=0)]
    unnamed x3 -> x2, local copies, waits for them, and re-layouts: 0.94 us -> 0.01 us
    pad x1 -> x0, local copies, waits for them, and re-layouts: 0.66 us -> none  [shards(): jnp.pad(partial_sum.reshape(devices, 1, rows), ((0, 0), (0, SUBLANES - 1)...]
where the time goes in v1:
time: 33.6 us; the launch traced here: 33.5 us
  Pallas kernels  32.3 us (96%)
  other arithmetic  1.11 us (3%)
    pallas_call x1, Pallas kernels, half_shards(): pl.pallas_call(functools.partial(half_kernel, depth_count, blk_count, row...  32.3 us
    sub x1, other arithmetic, half_shards(): return variance - quadratic[0, :rows]  1.11 us

profile of v1, /device:TPU:0, one launch (start us, length us, event | category | flops | bytes accessed | tf_op | source)
XLA Modules:
  0.0 33.5 jit_solution(1401837383643539497)
XLA Ops:
  0.0 0.0 copy-start
  0.0 32.3 %shard_map.37 = f32[1,128]{1,0:T(1,128)} custom-call(bf16[3,16384]{1,0:T(4,128)(2,1)} %jac_ref.1, bf16[4096,2048]{1,0:T(8,128)(2,1)} %gain_ref.1), custom_call_target="tpu_custom_call" | custom-call | tf_op jit(solution)/shard_map/pallas_call | solution.py:411
  32.4 0.0 copy-done
  32.4 1.1 %bitcast_subtract_fusion = f32[3]{0:T(128)} fusion(f32[3]{0:T(128)S(1)} %copy-done, f32[1,128]{1,0:T(1,128)} %shard_map.37), kind=kLoop, calls=%fused_computation | loop fusion | flops 3 | bytes 36 | tf_op jit(solution)/shard_map/sub | solution.py:441
Async XLA Ops:
  0.0 32.4 %copy-start = (f32[3]{0:T(128)S(1)}, f32[3]{0:T(128)}, u32[]{:S(2)}) copy-start(f32[3]{0:T(128)} %param.5) | copy-start | bytes 40

commit v2 on v0

--- a/solution.py
+++ b/solution.py
@@ -9,6 +9,7 @@
 
 LANES = 128
 SUBLANES = 8
+PACKED = 16
 MESH = pl.DeviceIdType.MESH
 
 
@@ -97,7 +98,7 @@
     return jacobian.reshape(rows, parts, width // LANES, LANES).transpose(1, 0, 2, 3)
 
 
-def shards(jacobian, gain_inverse, variance):
+def plain_shards(jacobian, gain_inverse, variance):
     rows = jacobian.shape[0]
     depth_count = lax.axis_size("depth")
     blk_count = lax.axis_size("blk")
@@ -117,7 +118,433 @@
     return variance - quadratic
 
 
+def half_kernel(
+    depth_count, blk_count, rows, jac_ref, gain_ref, out_ref,
+    own_raw, own_wide, lines, other_in, panel_in, wide, gain, left, parts, outgoing, arrived,
+    local_sem, line_send, line_recv, other_send, other_recv,
+    panel_send, panel_recv, twin_send, twin_recv, last_send, last_recv, through_sem,
+):
+    per = blk_count // depth_count
+    planes = depth_count
+    group = depth_count * per
+    half_group = group // 2
+    devices = depth_count * blk_count
+    states = jac_ref.shape[1]
+    chunks = states // LANES
+    sub = states // blk_count // LANES
+    width = sub * LANES
+    pitch = rows * sub + 1
+    end = planes - 1
+    depth = lax.axis_index("depth")
+    blk = lax.axis_index("blk")
+    plane = blk // per
+    side = lax.rem(blk, per)
+    spot = depth * per + side
+    parity = lax.rem(depth, 2)
+    twin = depth + 1 - 2 * parity
+    seat = (depth // 2) * per + side
+    on_diagonal = plane == depth
+
+    def inside(z):
+        return (z > 0) & (z < end)
+
+    two_up = inside(plane + 2)
+    two_down = inside(plane - 2)
+
+    def wrap(value, count):
+        return jnp.where(value >= count, value - count, value)
+
+    def other_section(d, z, s):
+        return d * per + jnp.where(d < z, s, per - 1 - s)
+
+    my_other = other_section(depth, plane, side)
+
+    def section_of(source, section):
+        return lines.at[source, :, pl.ds(pl.multiple_of(section * sub, sub), sub), :]
+
+    def remote(src, dst, send_sem, recv_sem, d, b):
+        return pltpu.make_async_remote_copy(
+            src_ref=src, dst_ref=dst, send_sem=send_sem, recv_sem=recv_sem,
+            device_id={"depth": d, "blk": b}, device_id_type=MESH,
+        )
+
+    def settle(ref, sem):
+        pltpu.make_async_copy(ref, ref, sem).wait()
+
+    jac_copy = pltpu.make_async_copy(jac_ref, own_raw, local_sem.at[0])
+    jac_copy.start()
+    gain_other = pltpu.make_async_copy(
+        gain_ref.at[pl.ds(pl.multiple_of((my_other - depth * per) * width, width), width), :],
+        gain.at[0], local_sem.at[1],
+    )
+    gain_own = pltpu.make_async_copy(
+        gain_ref.at[pl.ds(pl.multiple_of(side * width, width), width), :], gain.at[1], local_sem.at[2]
+    )
+    gain_other.start()
+
+    @pl.when(on_diagonal)
+    def _():
+        gain_own.start()
+
+    barrier = pltpu.get_barrier_semaphore()
+
+    def greet(d, b):
+        pl.semaphore_signal(barrier, inc=1, device_id={"depth": d, "blk": b}, device_id_type=MESH)
+
+    @pl.when(plane < end)
+    def _():
+        greet(depth, blk + per)
+
+    @pl.when(inside(plane) & (plane + 2 <= end))
+    def _():
+        greet(depth, blk + 2 * per)
+
+    for s in range(1, group):
+        member = wrap(spot + s, group)
+        greet(member // per, plane * per + lax.rem(member, per))
+
+    jac_copy.wait()
+    for c in range(chunks):
+        own_wide[pl.ds(c, rows, stride=chunks), :] = own_raw[:, c * LANES : (c + 1) * LANES].astype(
+            jnp.float32
+        )
+    for r in range(rows):
+        lines[plane, r] = own_wide[r * chunks : (r + 1) * chunks, :].astype(jnp.bfloat16)
+
+    below = jnp.where(plane > 0, 1, 0) + jnp.where(two_down, 1, 0)
+    pl.semaphore_wait(barrier, group - 1 + below)
+
+    def along(source, part, target, send_sem):
+        piece = lines.at[source, :, pl.ds(pl.multiple_of(part * (per * sub), per * sub), per * sub), :]
+        return remote(piece, piece, send_sem, line_recv.at[source, part], depth, target * per + side)
+
+    def first_part(source, target):
+        relayed = jnp.where(
+            (target == 0) & (source > 1), 1, jnp.where((target == end) & (source < end - 1), end - 1, target)
+        )
+        return wrap(relayed, planes)
+
+    def send_line(target, sem_at):
+        @pl.loop(0, planes)
+        def _(k):
+            part = wrap(first_part(plane, target) + k, planes)
+            along(plane, part, target, line_send.at[sem_at]).start()
+
+    def to_other(source, d, s):
+        receiver = d * per + s
+        seen = spot - receiver
+        seen = jnp.where(seen < 0, seen + group, seen)
+        return remote(
+            section_of(source, other_section(d, plane, s)), other_in.at[source, seen],
+            other_send.at[0], other_recv.at[source], d, plane * per + s,
+        )
+
+    def to_panel(source, step):
+        target = wrap(seat + step, half_group)
+        s = lax.rem(target, per)
+        return remote(
+            section_of(source, plane * per + s), panel_in.at[source, 0, half_group - step],
+            panel_send.at[0], panel_recv.at[source], (target // per) * 2 + parity, plane * per + s,
+        )
+
+    def own_to_twin(source):
+        return remote(
+            section_of(source, blk), panel_in.at[source, 1, 0],
+            twin_send.at[0], twin_recv.at[source], twin, blk,
+        )
+
+    def pass_to_twin(source):
+        return remote(
+            panel_in.at[source, 0, pl.ds(1, half_group - 1)], panel_in.at[source, 1, pl.ds(1, half_group - 1)],
+            twin_send.at[0], twin_recv.at[source], twin, blk,
+        )
+
+    def spread(source, part):
+        @pl.when(part == plane)
+        def _():
+            for step in range(1, half_group):
+                to_panel(source, step).start()
+            own_to_twin(source).start()
+
+        for s in range(per):
+            @pl.when((part != depth) | (side != s))
+            def _():
+                to_other(source, part, s).start()
+
+    def forward_panel(source):
+        settle(panel_in.at[source, 0, pl.ds(1, half_group - 1)], panel_recv.at[source])
+        pass_to_twin(source).start()
+
+    def tell(kind, b):
+        pl.semaphore_signal(
+            through_sem.at[kind], inc=1, device_id={"depth": depth, "blk": b}, device_id_type=MESH
+        )
+
+    @pl.when(plane > 0)
+    def _():
+        tell(0, blk - per)
+
+    @pl.when(two_down)
+    def _():
+        send_line(plane - 2, 1)
+
+    @pl.when(plane > 0)
+    def _():
+        send_line(plane - 1, 3)
+
+    @pl.loop(0, planes)
+    def _(k):
+        spread(plane, wrap(plane + k, planes))
+
+    @pl.when(plane < end)
+    def _():
+        pl.semaphore_wait(through_sem.at[0], 1)
+
+    @pl.when((plane > 0) & inside(plane + 1))
+    def _():
+        tell(1, blk - per)
+
+    @pl.when(two_up)
+    def _():
+        pl.semaphore_wait(through_sem.at[1], 1)
+        send_line(plane + 2, 0)
+
+    @pl.when(plane < end)
+    def _():
+        send_line(plane + 1, 2)
+
+    def relays(source):
+        down = (plane == 1) & (source > 1)
+        up = (plane == end - 1) & (source < end - 1)
+        return down, up
+
+    def stages(act):
+        for distance in range(1, planes):
+            @pl.when(plane - distance >= 0)
+            def _():
+                act(plane - distance)
+
+            @pl.when(plane + distance < planes)
+            def _():
+                act(plane + distance)
+
+    def receive(source):
+        down, up = relays(source)
+
+        @pl.loop(0, planes)
+        def _(k):
+            part = wrap(first_part(source, plane) + k, planes)
+            along(source, part, plane, line_send.at[0]).wait_recv()
+
+            @pl.when(down | up)
+            def _():
+                along(source, part, jnp.where(down, 0, end), line_send.at[4 + source]).start()
+
+            spread(source, part)
+
+    stages(receive)
+    forward_panel(plane)
+    stages(forward_panel)
+
+    def widen(index, slot, block):
+        wide[index, pl.ds(slot * pitch, rows * sub), :] = block.reshape(rows * sub, LANES).astype(
+            jnp.float32
+        )
+
+    def slot_of(source, d, s):
+        return d * blk_count + source * per + s
+
+    def collect(source):
+        slot = slot_of(source, depth, side)
+        widen(0, slot, section_of(source, my_other)[...])
+        widen(1, slot, section_of(source, blk)[...])
+
+        @pl.loop(1, half_group)
+        def _(k):
+            at = wrap(seat + k, half_group)
+            widen(1, slot_of(source, (at // per) * 2 + parity, lax.rem(at, per)), panel_in[source, 0, k])
+
+        settle(other_in.at[source, pl.ds(1, group - 1)], other_recv.at[source])
+
+        @pl.loop(1, group)
+        def _(k):
+            member = wrap(spot + k, group)
+            widen(0, slot_of(source, member // per, lax.rem(member, per)), other_in[source, k])
+
+        settle(panel_in.at[source, 1], twin_recv.at[source])
+
+        @pl.loop(0, half_group)
+        def _(k):
+            at = wrap(seat + k, half_group)
+            widen(1, slot_of(source, (at // per) * 2 + 1 - parity, lax.rem(at, per)), panel_in[source, 1, k])
+
+    collect(plane)
+    stages(collect)
+
+    def columns(index, c):
+        return [wide[index, pl.ds(r * sub + c, devices, stride=pitch), :] for r in range(rows)]
+
+    def narrow(index):
+        for c in range(sub):
+            for r, block in enumerate(columns(index, c)):
+                left[index, r * devices : (r + 1) * devices, c * LANES : (c + 1) * LANES] = block.astype(
+                    jnp.bfloat16
+                )
+
+    narrow(0)
+    block_width = width // 4
+    blocks = width // block_width
+    inner = block_width // LANES
+
+    def times_panel(total, product, n):
+        for c in range(inner):
+            panel = columns(1, n * inner + c)
+            for r in range(rows):
+                total[r] += product[r * devices : (r + 1) * devices, c * LANES : (c + 1) * LANES] * panel[r]
+
+    def dot(index, first, count, n):
+        if isinstance(first, int):
+            a = left[index, :, first : first + count]
+        else:
+            a = left[index, :, pl.ds(pl.multiple_of(first, LANES), count)]
+        b = gain[index, pl.ds(first, count), n * block_width : (n + 1) * block_width]
+        return jnp.dot(a, b, preferred_element_type=jnp.float32)
+
+    def zeros():
+        return [jnp.zeros((devices, LANES), jnp.float32) for _ in range(rows)]
+
+    gain_other.wait()
+
+    @pl.when(jnp.logical_not(on_diagonal))
+    def _():
+        total = zeros()
+        for n in range(blocks):
+            times_panel(total, dot(0, 0, width, n), n)
+        for r in range(rows):
+            parts[r] = total[r] * 2.0
+
+    @pl.when(on_diagonal)
+    def _():
+        narrow(1)
+        gain_own.wait()
+        total = zeros()
+        for n in range(blocks):
+            later = 1 if 2 * n >= blocks else 0
+            quarter = jnp.where(side == 0, later, 1 - later) * (width // 2)
+            product = dot(0, quarter, width // 2, n)
+            if n:
+                product += dot(1, 0, n * block_width, n)
+            product = product * 2.0 + dot(1, n * block_width, block_width, n)
+            times_panel(total, product, n)
+        for r in range(rows):
+            parts[r] = total[r]
+
+    lane = lax.broadcasted_iota(jnp.int32, (devices, LANES), 1)
+    packed = jnp.zeros((devices, LANES), jnp.float32)
+    for r in range(rows):
+        packed = jnp.where(lane == r, jnp.sum(parts[r], axis=1, keepdims=True), packed)
+    for t in range(devices):
+        outgoing[t] = packed[t : t + 1]
+
+    def last(dd, db):
+        d, b = depth ^ dd, blk ^ db
+        return remote(
+            outgoing.at[d * blk_count + b], arrived.at[dd * blk_count + db],
+            last_send.at[0], last_recv.at[0], d, b,
+        )
+
+    for db in reversed(range(blk_count)):
+        for dd in reversed(range(depth_count)):
+            if dd or db:
+                last(dd, db).start()
+
+    own = outgoing[depth * blk_count + blk]
+
+    for sem_at, cond in enumerate((two_up, two_down, plane < end, plane > 0)):
+        @pl.when(cond)
+        def _():
+            settle(lines.at[0], line_send.at[sem_at])
+
+    def relayed(source):
+        down, up = relays(source)
+
+        @pl.when(down | up)
+        def _():
+            settle(lines.at[0], line_send.at[4 + source])
+
+    stages(relayed)
+    settle(other_in.at[:, pl.ds(1, group - 1)], other_send.at[0])
+    settle(panel_in.at[:, 0, pl.ds(1, half_group - 1)], panel_send.at[0])
+    settle(panel_in.at[:, 1], twin_send.at[0])
+    settle(arrived.at[pl.ds(1, devices - 1)], last_send.at[0])
+    settle(arrived.at[pl.ds(1, devices - 1)], last_recv.at[0])
+
+    total = own
+    for t in range(1, devices):
+        total += arrived[t]
+    out_ref[...] = total
+
+
+def half_shards(jacobian, gain_inverse, variance):
+    rows, states = jacobian.shape
+    depth_count = lax.axis_size("depth")
+    blk_count = lax.axis_size("blk")
+    devices = depth_count * blk_count
+    per = blk_count // depth_count
+    planes, group = depth_count, depth_count * per
+    chunks = states // LANES
+    sub = states // blk_count // LANES
+    width = sub * LANES
+    bf16, f32 = jnp.bfloat16, jnp.float32
+    dma = pltpu.SemaphoreType.DMA
+    quadratic = pl.pallas_call(
+        functools.partial(half_kernel, depth_count, blk_count, rows),
+        out_shape=jax.ShapeDtypeStruct((1, LANES), f32),
+        in_specs=[pl.BlockSpec(memory_space=pl.ANY)] * 2,
+        out_specs=pl.BlockSpec(memory_space=pltpu.VMEM),
+        scratch_shapes=[
+            pltpu.VMEM((rows, states), bf16),
+            pltpu.VMEM((rows * chunks, LANES), f32),
+            pltpu.VMEM((planes, rows, chunks, LANES), bf16),
+            pltpu.VMEM((planes, group, rows, sub, LANES), bf16),
+            pltpu.VMEM((planes, 2, group // 2, rows, sub, LANES), bf16),
+            pltpu.VMEM((2, devices * (rows * sub + 1), LANES), f32),
+            pltpu.VMEM((2, width, width), bf16),
+            pltpu.VMEM((2, rows * devices, width), bf16),
+            pltpu.VMEM((rows, devices, LANES), f32),
+            pltpu.VMEM((devices, 1, LANES), f32),
+            pltpu.VMEM((devices, 1, LANES), f32),
+            dma((3,)),
+            dma((4 + planes,)),
+            dma((planes, planes)),
+            dma((1,)),
+            dma((planes,)),
+            dma((1,)),
+            dma((planes,)),
+            dma((1,)),
+            dma((planes,)),
+            dma((1,)),
+            dma((1,)),
+            pltpu.SemaphoreType.REGULAR((2,)),
+        ],
+        compiler_params=pltpu.CompilerParams(
+            collective_id=0, has_side_effects=True, vmem_limit_bytes=60 * 1024 * 1024
+        ),
+    )(jacobian, gain_inverse)
+    return variance - quadratic[0, :rows]
+
+
 def solution(mesh):
     in_specs = (P(("depth", "blk"), None), P("depth", "blk"), P(("depth", "blk")))
     out_specs = P(("depth", "blk"))
+    depth_count, blk_count = mesh.shape["depth"], mesh.shape["blk"]
+
+    def shards(jacobian, gain_inverse, variance):
+        width = gain_inverse.shape[1]
+        fits = gain_inverse.size * gain_inverse.dtype.itemsize <= 16 * 1024 * 1024
+        paired = depth_count in (2, 4) and blk_count == 2 * depth_count
+        if paired and width % (PACKED * LANES) == 0 and fits:
+            return half_shards(jacobian, gain_inverse, variance)
+        return plain_shards(jacobian, gain_inverse, variance)
+
     return jax.shard_map(shards, mesh=mesh, in_specs=in_specs, out_specs=out_specs, check_vma=False)

time: 61.8 us -> 28.9 us (0.47)
  Pallas kernels: 46.9 us -> 27.6 us
  matrix products: 9.1 us -> 0 us
  local copies, waits for them, and re-layouts: 2.98 us -> 0.01 us
  other arithmetic: 2.53 us -> 1.11 us
    pallas_call x2 -> x1, Pallas kernels: 46.9 us -> 27.6 us  [half_shards(): pl.pallas_call(functools.partial(half_kernel, depth_count, blk_count, row...]
    dot_general x1 -> x0, matrix products: 9.1 us -> none  [shards(): projected = jnp.dot(left, gain_inverse, preferred_element_type=jnp.float32)]
    reshape x3 -> x0, local copies, waits for them, and re-layouts: 1.38 us -> none  [the longest x2 1.28 us: sections(): jacobian.reshape(rows, parts, width // LANES, LANES).transpose(1, 0, 2, 3)]
    unnamed x1 -> x0, other arithmetic: 1.06 us -> none
    reduce_sum x1 -> x0, other arithmetic: 0.96 us -> none  [shards(): quadratic = jnp.sum(gathered[:, 0, :rows], axis=0)]
    unnamed x3 -> x2, local copies, waits for them, and re-layouts: 0.94 us -> 0.01 us
    pad x1 -> x0, local copies, waits for them, and re-layouts: 0.66 us -> none  [shards(): jnp.pad(partial_sum.reshape(devices, 1, rows), ((0, 0), (0, SUBLANES - 1)...]
where the time goes in v2:
time: 28.9 us; the launch traced here: 28.8 us
  Pallas kernels  27.6 us (96%)
  other arithmetic  1.11 us (4%)
    pallas_call x1, Pallas kernels, half_shards(): pl.pallas_call(functools.partial(half_kernel, depth_count, blk_count, row...  27.6 us
    sub x1, other arithmetic, half_shards(): return variance - quadratic[0, :rows]  1.11 us

profile of v2, /device:TPU:0, one launch (start us, length us, event | category | flops | bytes accessed | tf_op | source)
XLA Modules:
  0.0 28.8 jit_solution(5765237772582470)
XLA Ops:
  0.0 0.0 copy-start
  0.0 27.6 %shard_map.37 = f32[1,128]{1,0:T(1,128)} custom-call(bf16[3,16384]{1,0:T(4,128)(2,1)} %jac_ref.1, bf16[4096,2048]{1,0:T(8,128)(2,1)} %gain_ref.1), custom_call_target="tpu_custom_call" | custom-call | tf_op jit(solution)/shard_map/pallas_call | solution.py:500
  27.6 0.0 copy-done
  27.6 1.1 %bitcast_subtract_fusion = f32[3]{0:T(128)} fusion(f32[3]{0:T(128)S(1)} %copy-done, f32[1,128]{1,0:T(1,128)} %shard_map.37), kind=kLoop, calls=%fused_computation | loop fusion | flops 3 | bytes 36 | tf_op jit(solution)/shard_map/sub | solution.py:534
Async XLA Ops:
  0.0 27.6 %copy-start = (f32[3]{0:T(128)S(1)}, f32[3]{0:T(128)}, u32[]{:S(2)}) copy-start(f32[3]{0:T(128)} %param.5) | copy-start | bytes 40

commit v3 on v2

--- a/solution.py
+++ b/solution.py
@@ -120,9 +120,9 @@
 
 def half_kernel(
     depth_count, blk_count, rows, jac_ref, gain_ref, out_ref,
-    own_raw, own_wide, lines, other_in, panel_in, wide, gain, left, parts, outgoing, arrived,
+    own_raw, own_wide, lines, other_in, panel_in, wide, gain, left, projected, outgoing, arrived,
     local_sem, line_send, line_recv, other_send, other_recv,
-    panel_send, panel_recv, twin_send, twin_recv, last_send, last_recv, through_sem,
+    panel_send, panel_recv, twin_send, twin_recv, last_send, last_recv,
 ):
     per = blk_count // depth_count
     planes = depth_count
@@ -191,17 +191,18 @@
     def greet(d, b):
         pl.semaphore_signal(barrier, inc=1, device_id={"depth": d, "blk": b}, device_id_type=MESH)
 
-    @pl.when(plane < end)
-    def _():
-        greet(depth, blk + per)
-
-    @pl.when(inside(plane) & (plane + 2 <= end))
-    def _():
-        greet(depth, blk + 2 * per)
-
     for s in range(1, group):
         member = wrap(spot + s, group)
         greet(member // per, plane * per + lax.rem(member, per))
+
+    for away in (1, -1, 2, -2):
+        known = (plane + away >= 0) & (plane + away <= end)
+        if abs(away) == 2:
+            known = known & inside(plane)
+
+        @pl.when(known)
+        def _():
+            greet(depth, blk + away * per)
 
     jac_copy.wait()
     for c in range(chunks):
@@ -211,8 +212,10 @@
     for r in range(rows):
         lines[plane, r] = own_wide[r * chunks : (r + 1) * chunks, :].astype(jnp.bfloat16)
 
-    below = jnp.where(plane > 0, 1, 0) + jnp.where(two_down, 1, 0)
-    pl.semaphore_wait(barrier, group - 1 + below)
+    heard = group - 1
+    for known in (plane > 0, plane < end, two_up, two_down):
+        heard = heard + jnp.where(known, 1, 0)
+    pl.semaphore_wait(barrier, heard)
 
     def along(source, part, target, send_sem):
         piece = lines.at[source, :, pl.ds(pl.multiple_of(part * (per * sub), per * sub), per * sub), :]
@@ -275,43 +278,14 @@
         settle(panel_in.at[source, 0, pl.ds(1, half_group - 1)], panel_recv.at[source])
         pass_to_twin(source).start()
 
-    def tell(kind, b):
-        pl.semaphore_signal(
-            through_sem.at[kind], inc=1, device_id={"depth": depth, "blk": b}, device_id_type=MESH
-        )
-
-    @pl.when(plane > 0)
-    def _():
-        tell(0, blk - per)
-
-    @pl.when(two_down)
-    def _():
-        send_line(plane - 2, 1)
-
-    @pl.when(plane > 0)
-    def _():
-        send_line(plane - 1, 3)
+    for sem_at, known, away in ((1, two_down, -2), (3, plane > 0, -1), (2, plane < end, 1), (0, two_up, 2)):
+        @pl.when(known)
+        def _():
+            send_line(plane + away, sem_at)
 
     @pl.loop(0, planes)
     def _(k):
         spread(plane, wrap(plane + k, planes))
-
-    @pl.when(plane < end)
-    def _():
-        pl.semaphore_wait(through_sem.at[0], 1)
-
-    @pl.when((plane > 0) & inside(plane + 1))
-    def _():
-        tell(1, blk - per)
-
-    @pl.when(two_up)
-    def _():
-        pl.semaphore_wait(through_sem.at[1], 1)
-        send_line(plane + 2, 0)
-
-    @pl.when(plane < end)
-    def _():
-        send_line(plane + 1, 2)
 
     def relays(source):
         down = (plane == 1) & (source > 1)
@@ -319,14 +293,13 @@
         return down, up
 
     def stages(act):
-        for distance in range(1, planes):
-            @pl.when(plane - distance >= 0)
-            def _():
-                act(plane - distance)
-
-            @pl.when(plane + distance < planes)
-            def _():
-                act(plane + distance)
+        for way in (-1, 1):
+            for distance in range(1, planes):
+                source = plane + way * distance
+
+                @pl.when((source >= 0) & (source <= end))
+                def _():
+                    act(source)
 
     def receive(source):
         down, up = relays(source)
@@ -343,8 +316,6 @@
             spread(source, part)
 
     stages(receive)
-    forward_panel(plane)
-    stages(forward_panel)
 
     def widen(index, slot, block):
         wide[index, pl.ds(slot * pitch, rows * sub), :] = block.reshape(rows * sub, LANES).astype(
@@ -354,16 +325,8 @@
     def slot_of(source, d, s):
         return d * blk_count + source * per + s
 
-    def collect(source):
-        slot = slot_of(source, depth, side)
-        widen(0, slot, section_of(source, my_other)[...])
-        widen(1, slot, section_of(source, blk)[...])
-
-        @pl.loop(1, half_group)
-        def _(k):
-            at = wrap(seat + k, half_group)
-            widen(1, slot_of(source, (at // per) * 2 + parity, lax.rem(at, per)), panel_in[source, 0, k])
-
+    def collect_other(source):
+        widen(0, slot_of(source, depth, side), section_of(source, my_other)[...])
         settle(other_in.at[source, pl.ds(1, group - 1)], other_recv.at[source])
 
         @pl.loop(1, group)
@@ -371,6 +334,8 @@
             member = wrap(spot + k, group)
             widen(0, slot_of(source, member // per, lax.rem(member, per)), other_in[source, k])
 
+    def collect_panel(source):
+        widen(1, slot_of(source, depth, side), section_of(source, blk)[...])
         settle(panel_in.at[source, 1], twin_recv.at[source])
 
         @pl.loop(0, half_group)
@@ -378,8 +343,14 @@
             at = wrap(seat + k, half_group)
             widen(1, slot_of(source, (at // per) * 2 + 1 - parity, lax.rem(at, per)), panel_in[source, 1, k])
 
-    collect(plane)
-    stages(collect)
+            @pl.when(k > 0)
+            def _():
+                widen(1, slot_of(source, (at // per) * 2 + parity, lax.rem(at, per)), panel_in[source, 0, k])
+
+    collect_other(plane)
+    stages(collect_other)
+    forward_panel(plane)
+    stages(forward_panel)
 
     def columns(index, c):
         return [wide[index, pl.ds(r * sub + c, devices, stride=pitch), :] for r in range(rows)]
@@ -395,12 +366,6 @@
     block_width = width // 4
     blocks = width // block_width
     inner = block_width // LANES
-
-    def times_panel(total, product, n):
-        for c in range(inner):
-            panel = columns(1, n * inner + c)
-            for r in range(rows):
-                total[r] += product[r * devices : (r + 1) * devices, c * LANES : (c + 1) * LANES] * panel[r]
 
     def dot(index, first, count, n):
         if isinstance(first, int):
@@ -410,39 +375,42 @@
         b = gain[index, pl.ds(first, count), n * block_width : (n + 1) * block_width]
         return jnp.dot(a, b, preferred_element_type=jnp.float32)
 
-    def zeros():
-        return [jnp.zeros((devices, LANES), jnp.float32) for _ in range(rows)]
-
     gain_other.wait()
 
     @pl.when(jnp.logical_not(on_diagonal))
     def _():
-        total = zeros()
         for n in range(blocks):
-            times_panel(total, dot(0, 0, width, n), n)
-        for r in range(rows):
-            parts[r] = total[r] * 2.0
+            projected[:, n * block_width : (n + 1) * block_width] = dot(0, 0, width, n)
+
+    @pl.when(on_diagonal)
+    def _():
+        for n in range(blocks):
+            later = 1 if 2 * n >= blocks else 0
+            quarter = jnp.where(side == 0, later, 1 - later) * (width // 2)
+            projected[:, n * block_width : (n + 1) * block_width] = dot(0, quarter, width // 2, n)
+
+    collect_panel(plane)
+    stages(collect_panel)
 
     @pl.when(on_diagonal)
     def _():
         narrow(1)
         gain_own.wait()
-        total = zeros()
         for n in range(blocks):
-            later = 1 if 2 * n >= blocks else 0
-            quarter = jnp.where(side == 0, later, 1 - later) * (width // 2)
-            product = dot(0, quarter, width // 2, n)
+            at = slice(n * block_width, (n + 1) * block_width)
             if n:
-                product += dot(1, 0, n * block_width, n)
-            product = product * 2.0 + dot(1, n * block_width, block_width, n)
-            times_panel(total, product, n)
-        for r in range(rows):
-            parts[r] = total[r]
+                projected[:, at] += dot(1, 0, n * block_width, n)
+            projected[:, at] += dot(1, n * block_width, block_width, n) * 0.5
+
+    total = [jnp.zeros((devices, LANES), jnp.float32) for _ in range(rows)]
+    for c in range(sub):
+        for r, panel in enumerate(columns(1, c)):
+            total[r] += projected[r * devices : (r + 1) * devices, c * LANES : (c + 1) * LANES] * panel
 
     lane = lax.broadcasted_iota(jnp.int32, (devices, LANES), 1)
     packed = jnp.zeros((devices, LANES), jnp.float32)
     for r in range(rows):
-        packed = jnp.where(lane == r, jnp.sum(parts[r], axis=1, keepdims=True), packed)
+        packed = jnp.where(lane == r, 2.0 * jnp.sum(total[r], axis=1, keepdims=True), packed)
     for t in range(devices):
         outgoing[t] = packed[t : t + 1]
 
@@ -479,10 +447,10 @@
     settle(arrived.at[pl.ds(1, devices - 1)], last_send.at[0])
     settle(arrived.at[pl.ds(1, devices - 1)], last_recv.at[0])
 
-    total = own
+    whole = own
     for t in range(1, devices):
-        total += arrived[t]
-    out_ref[...] = total
+        whole += arrived[t]
+    out_ref[...] = whole
 
 
 def half_shards(jacobian, gain_inverse, variance):
@@ -511,7 +479,7 @@
             pltpu.VMEM((2, devices * (rows * sub + 1), LANES), f32),
             pltpu.VMEM((2, width, width), bf16),
             pltpu.VMEM((2, rows * devices, width), bf16),
-            pltpu.VMEM((rows, devices, LANES), f32),
+            pltpu.VMEM((rows * devices, width), f32),
             pltpu.VMEM((devices, 1, LANES), f32),
             pltpu.VMEM((devices, 1, LANES), f32),
             dma((3,)),
@@ -525,7 +493,6 @@
             dma((planes,)),
             dma((1,)),
             dma((1,)),
-            pltpu.SemaphoreType.REGULAR((2,)),
         ],
         compiler_params=pltpu.CompilerParams(
             collective_id=0, has_side_effects=True, vmem_limit_bytes=60 * 1024 * 1024

time: 28.9 us -> 26.6 us (0.920)
  Pallas kernels: 27.6 us -> 25.3 us
    pallas_call x1, Pallas kernels: 27.6 us -> 25.3 us  [half_shards(): pl.pallas_call(functools.partial(half_kernel, depth_count, blk_count, row...]
where the time goes in v3:
time: 26.6 us; the launch traced here: 26.5 us
  Pallas kernels  25.3 us (95%)
  other arithmetic  1.11 us (4%)
    pallas_call x1, Pallas kernels, half_shards(): pl.pallas_call(functools.partial(half_kernel, depth_count, blk_count, row...  25.3 us
    sub x1, other arithmetic, half_shards(): return variance - quadratic[0, :rows]  1.11 us

profile of v3, /device:TPU:0, one launch (start us, length us, event | category | flops | bytes accessed | tf_op | source)
XLA Modules:
  0.0 26.5 jit_solution(13891610945639174428)
XLA Ops:
  0.0 0.0 copy-start
  0.0 25.3 %shard_map.37 = f32[1,128]{1,0:T(1,128)} custom-call(bf16[3,16384]{1,0:T(4,128)(2,1)} %jac_ref.1, bf16[4096,2048]{1,0:T(8,128)(2,1)} %gain_ref.1), custom_call_target="tpu_custom_call" | custom-call | tf_op jit(solution)/shard_map/pallas_call | solution.py:468
  25.3 0.0 copy-done
  25.3 1.1 %bitcast_subtract_fusion = f32[3]{0:T(128)} fusion(f32[3]{0:T(128)S(1)} %copy-done, f32[1,128]{1,0:T(1,128)} %shard_map.37), kind=kLoop, calls=%fused_computation | loop fusion | flops 3 | bytes 36 | tf_op jit(solution)/shard_map/sub | solution.py:501
Async XLA Ops:
  0.0 25.3 %copy-start = (f32[3]{0:T(128)S(1)}, f32[3]{0:T(128)}, u32[]{:S(2)}) copy-start(f32[3]{0:T(128)} %param.5) | copy-start | bytes 40

commit v4 on v3

--- a/solution.py
+++ b/solution.py
@@ -120,7 +120,7 @@
 
 def half_kernel(
     depth_count, blk_count, rows, jac_ref, gain_ref, out_ref,
-    own_raw, own_wide, lines, other_in, panel_in, wide, gain, left, projected, outgoing, arrived,
+    own_raw, own_wide, lines, other_in, panel_in, wide, gain, left, projected, partial, outgoing, arrived,
     local_sem, line_send, line_recv, other_send, other_recv,
     panel_send, panel_recv, twin_send, twin_recv, last_send, last_recv,
 ):
@@ -145,6 +145,23 @@
     seat = (depth // 2) * per + side
     on_diagonal = plane == depth
 
+    def at_end(z):
+        return (z == 0) | (z == end)
+
+    def adjacent(d, z):
+        return (d - z == 1) | (z - d == 1)
+
+    def takes_none(d, z):
+        return adjacent(d, z) & at_end(z)
+
+    def takes_both(d, z):
+        return adjacent(d, z) & at_end(d)
+
+    idle = takes_none(depth, plane)
+    double = takes_both(depth, plane)
+    single = jnp.logical_not(idle | double)
+    sources = [jnp.where(i < plane, plane - 1 - i, i + 1) for i in range(planes - 1)]
+
     def inside(z):
         return (z > 0) & (z < end)
 
@@ -173,18 +190,22 @@
 
     jac_copy = pltpu.make_async_copy(jac_ref, own_raw, local_sem.at[0])
     jac_copy.start()
-    gain_other = pltpu.make_async_copy(
-        gain_ref.at[pl.ds(pl.multiple_of((my_other - depth * per) * width, width), width), :],
+    gain_first = pltpu.make_async_copy(
+        gain_ref.at[pl.ds(pl.multiple_of(jnp.where(double, 0, my_other - depth * per) * width, width), width), :],
         gain.at[0], local_sem.at[1],
     )
-    gain_own = pltpu.make_async_copy(
-        gain_ref.at[pl.ds(pl.multiple_of(side * width, width), width), :], gain.at[1], local_sem.at[2]
+    gain_second = pltpu.make_async_copy(
+        gain_ref.at[pl.ds(pl.multiple_of(jnp.where(double, 1, side) * width, width), width), :],
+        gain.at[1], local_sem.at[2],
     )
-    gain_other.start()
-
-    @pl.when(on_diagonal)
-    def _():
-        gain_own.start()
+
+    @pl.when(jnp.logical_not(idle))
+    def _():
+        gain_first.start()
+
+    @pl.when(on_diagonal | double)
+    def _():
+        gain_second.start()
 
     barrier = pltpu.get_barrier_semaphore()
 
@@ -221,25 +242,33 @@
         piece = lines.at[source, :, pl.ds(pl.multiple_of(part * (per * sub), per * sub), per * sub), :]
         return remote(piece, piece, send_sem, line_recv.at[source, part], depth, target * per + side)
 
-    def first_part(source, target):
-        relayed = jnp.where(
-            (target == 0) & (source > 1), 1, jnp.where((target == end) & (source < end - 1), end - 1, target)
-        )
-        return wrap(relayed, planes)
+    def first_part(target):
+        return wrap(jnp.clip(target, 1, end - 1) + 1, planes)
+
+    def part_count(target):
+        return jnp.where(at_end(target), planes - 1, planes)
 
     def send_line(target, sem_at):
-        @pl.loop(0, planes)
+        @pl.loop(0, part_count(target))
         def _(k):
-            part = wrap(first_part(plane, target) + k, planes)
-            along(plane, part, target, line_send.at[sem_at]).start()
+            along(plane, wrap(first_part(target) + k, planes), target, line_send.at[sem_at]).start()
+
+    def seen_from(d, s):
+        seen = spot - (d * per + s)
+        return jnp.where(seen < 0, seen + group, seen)
 
     def to_other(source, d, s):
-        receiver = d * per + s
-        seen = spot - receiver
-        seen = jnp.where(seen < 0, seen + group, seen)
         return remote(
-            section_of(source, other_section(d, plane, s)), other_in.at[source, seen],
-            other_send.at[0], other_recv.at[source], d, plane * per + s,
+            section_of(source, other_section(d, plane, s)),
+            other_in.at[source, seen_from(d, s), :, pl.ds(0, sub)],
+            other_send.at[d], other_recv.at[source], d, plane * per + s,
+        )
+
+    def to_both(source, d, s):
+        return remote(
+            lines.at[source, :, pl.ds(pl.multiple_of(d * per * sub, per * sub), per * sub), :],
+            other_in.at[source, seen_from(d, s)],
+            other_send.at[d], other_recv.at[source], d, plane * per + s,
         )
 
     def to_panel(source, step):
@@ -270,7 +299,13 @@
             own_to_twin(source).start()
 
         for s in range(per):
-            @pl.when((part != depth) | (side != s))
+            foreign = (part != depth) | (side != s)
+
+            @pl.when(foreign & takes_both(part, plane))
+            def _():
+                to_both(source, part, s).start()
+
+            @pl.when(foreign & jnp.logical_not(adjacent(part, plane) & (at_end(part) | at_end(plane))))
             def _():
                 to_other(source, part, s).start()
 
@@ -292,30 +327,31 @@
         up = (plane == end - 1) & (source < end - 1)
         return down, up
 
-    def stages(act):
-        for way in (-1, 1):
-            for distance in range(1, planes):
-                source = plane + way * distance
-
-                @pl.when((source >= 0) & (source <= end))
-                def _():
-                    act(source)
-
-    def receive(source):
+    def receive(source, k):
         down, up = relays(source)
-
-        @pl.loop(0, planes)
-        def _(k):
-            part = wrap(first_part(source, plane) + k, planes)
-            along(source, part, plane, line_send.at[0]).wait_recv()
-
-            @pl.when(down | up)
-            def _():
-                along(source, part, jnp.where(down, 0, end), line_send.at[4 + source]).start()
-
-            spread(source, part)
-
-    stages(receive)
+        part = wrap(first_part(plane) + k, planes)
+        along(source, part, plane, line_send.at[0]).wait_recv()
+
+        @pl.when((down | up) & (k < planes - 1))
+        def _():
+            along(source, part, jnp.where(down, 0, end), line_send.at[4 + source]).start()
+
+        spread(source, part)
+
+    @pl.when(at_end(plane))
+    def _():
+        for source in sources:
+            @pl.loop(0, planes - 1)
+            def _(k):
+                receive(source, k)
+
+    @pl.when(jnp.logical_not(at_end(plane)))
+    def _():
+        for turn in (sources[:2], sources[2:]):
+            @pl.loop(0, planes)
+            def _(k):
+                for source in turn:
+                    receive(source, k)
 
     def widen(index, slot, block):
         wide[index, pl.ds(slot * pitch, rows * sub), :] = block.reshape(rows * sub, LANES).astype(
@@ -326,13 +362,27 @@
         return d * blk_count + source * per + s
 
     def collect_other(source):
-        widen(0, slot_of(source, depth, side), section_of(source, my_other)[...])
-        settle(other_in.at[source, pl.ds(1, group - 1)], other_recv.at[source])
-
-        @pl.loop(1, group)
-        def _(k):
-            member = wrap(spot + k, group)
-            widen(0, slot_of(source, member // per, lax.rem(member, per)), other_in[source, k])
+        slot = slot_of(source, depth, side)
+
+        def gather(first_section, count, indices):
+            settle(other_in.at[source, pl.ds(1, group - 1), :, pl.ds(0, count * sub)], other_recv.at[source])
+            for n, index in enumerate(indices):
+                widen(index, slot, section_of(source, first_section + n)[...])
+
+            @pl.loop(1, group)
+            def _(k):
+                member = wrap(spot + k, group)
+                at = slot_of(source, member // per, lax.rem(member, per))
+                for n, index in enumerate(indices):
+                    widen(index, at, other_in[source, k, :, n * sub : (n + 1) * sub])
+
+        @pl.when(single)
+        def _():
+            gather(my_other, 1, (0,))
+
+        @pl.when(double)
+        def _():
+            gather(depth * per, 2, (0, 2))
 
     def collect_panel(source):
         widen(1, slot_of(source, depth, side), section_of(source, blk)[...])
@@ -347,22 +397,22 @@
             def _():
                 widen(1, slot_of(source, (at // per) * 2 + parity, lax.rem(at, per)), panel_in[source, 0, k])
 
-    collect_other(plane)
-    stages(collect_other)
-    forward_panel(plane)
-    stages(forward_panel)
+    everything = [plane] + sources
+    for source in everything:
+        collect_other(source)
+    for source in everything:
+        forward_panel(source)
 
     def columns(index, c):
         return [wide[index, pl.ds(r * sub + c, devices, stride=pitch), :] for r in range(rows)]
 
-    def narrow(index):
+    def narrow(index, source):
         for c in range(sub):
-            for r, block in enumerate(columns(index, c)):
+            for r, block in enumerate(columns(source, c)):
                 left[index, r * devices : (r + 1) * devices, c * LANES : (c + 1) * LANES] = block.astype(
                     jnp.bfloat16
                 )
 
-    narrow(0)
     block_width = width // 4
     blocks = width // block_width
     inner = block_width // LANES
@@ -375,42 +425,63 @@
         b = gain[index, pl.ds(first, count), n * block_width : (n + 1) * block_width]
         return jnp.dot(a, b, preferred_element_type=jnp.float32)
 
-    gain_other.wait()
-
-    @pl.when(jnp.logical_not(on_diagonal))
+    def columns_of(n):
+        return slice(n * block_width, (n + 1) * block_width)
+
+    @pl.when(jnp.logical_not(idle))
+    def _():
+        narrow(0, 0)
+        gain_first.wait()
+
+    @pl.when(single & jnp.logical_not(on_diagonal))
     def _():
         for n in range(blocks):
-            projected[:, n * block_width : (n + 1) * block_width] = dot(0, 0, width, n)
+            projected[:, columns_of(n)] = dot(0, 0, width, n)
+
+    @pl.when(double)
+    def _():
+        narrow(1, 2)
+        gain_second.wait()
+        for n in range(blocks):
+            projected[:, columns_of(n)] = dot(0, 0, width, n) + dot(1, 0, width, n)
 
     @pl.when(on_diagonal)
     def _():
         for n in range(blocks):
             later = 1 if 2 * n >= blocks else 0
             quarter = jnp.where(side == 0, later, 1 - later) * (width // 2)
-            projected[:, n * block_width : (n + 1) * block_width] = dot(0, quarter, width // 2, n)
-
-    collect_panel(plane)
-    stages(collect_panel)
+            projected[:, columns_of(n)] = dot(0, quarter, width // 2, n)
+
+    for source in everything:
+        collect_panel(source)
 
     @pl.when(on_diagonal)
     def _():
-        narrow(1)
-        gain_own.wait()
+        narrow(1, 1)
+        gain_second.wait()
         for n in range(blocks):
-            at = slice(n * block_width, (n + 1) * block_width)
+            at = columns_of(n)
             if n:
                 projected[:, at] += dot(1, 0, n * block_width, n)
             projected[:, at] += dot(1, n * block_width, block_width, n) * 0.5
 
-    total = [jnp.zeros((devices, LANES), jnp.float32) for _ in range(rows)]
-    for c in range(sub):
-        for r, panel in enumerate(columns(1, c)):
-            total[r] += projected[r * devices : (r + 1) * devices, c * LANES : (c + 1) * LANES] * panel
+    @pl.when(idle)
+    def _():
+        partial[...] = jnp.zeros_like(partial)
+
+    @pl.when(jnp.logical_not(idle))
+    def _():
+        total = [jnp.zeros((devices, LANES), jnp.float32) for _ in range(rows)]
+        for c in range(sub):
+            for r, panel in enumerate(columns(1, c)):
+                total[r] += projected[r * devices : (r + 1) * devices, c * LANES : (c + 1) * LANES] * panel
+        for r in range(rows):
+            partial[r] = total[r]
 
     lane = lax.broadcasted_iota(jnp.int32, (devices, LANES), 1)
     packed = jnp.zeros((devices, LANES), jnp.float32)
     for r in range(rows):
-        packed = jnp.where(lane == r, 2.0 * jnp.sum(total[r], axis=1, keepdims=True), packed)
+        packed = jnp.where(lane == r, 2.0 * jnp.sum(partial[r], axis=1, keepdims=True), packed)
     for t in range(devices):
         outgoing[t] = packed[t : t + 1]
 
@@ -428,20 +499,30 @@
 
     own = outgoing[depth * blk_count + blk]
 
-    for sem_at, cond in enumerate((two_up, two_down, plane < end, plane > 0)):
-        @pl.when(cond)
-        def _():
-            settle(lines.at[0], line_send.at[sem_at])
-
-    def relayed(source):
+    def line_left(cond, target, sem):
+        @pl.when(cond & at_end(target))
+        def _():
+            settle(lines.at[0, :, pl.ds(0, (planes - 1) * per * sub)], sem)
+
+        @pl.when(cond & jnp.logical_not(at_end(target)))
+        def _():
+            settle(lines.at[0], sem)
+
+    for sem_at, known, away in ((1, two_down, -2), (3, plane > 0, -1), (2, plane < end, 1), (0, two_up, 2)):
+        line_left(known, plane + away, line_send.at[sem_at])
+
+    for source in sources:
         down, up = relays(source)
-
-        @pl.when(down | up)
-        def _():
-            settle(lines.at[0], line_send.at[4 + source])
-
-    stages(relayed)
-    settle(other_in.at[:, pl.ds(1, group - 1)], other_send.at[0])
+        line_left(down | up, 0, line_send.at[4 + source])
+
+    for d in range(depth_count):
+        for members, here in ((per - 1, depth == d), (per, depth != d)):
+            both = takes_both(d, plane)
+            for count, taken in ((2, both), (1, jnp.logical_not(both | takes_none(d, plane)))):
+                @pl.when(here & taken)
+                def _():
+                    settle(other_in.at[:, pl.ds(0, members), :, pl.ds(0, count * sub)], other_send.at[d])
+
     settle(panel_in.at[:, 0, pl.ds(1, half_group - 1)], panel_send.at[0])
     settle(panel_in.at[:, 1], twin_send.at[0])
     settle(arrived.at[pl.ds(1, devices - 1)], last_send.at[0])
@@ -467,25 +548,26 @@
     dma = pltpu.SemaphoreType.DMA
     quadratic = pl.pallas_call(
         functools.partial(half_kernel, depth_count, blk_count, rows),
-        out_shape=jax.ShapeDtypeStruct((1, LANES), f32),
+        out_shape=pltpu.VMEM((1, LANES), f32),
         in_specs=[pl.BlockSpec(memory_space=pl.ANY)] * 2,
         out_specs=pl.BlockSpec(memory_space=pltpu.VMEM),
         scratch_shapes=[
             pltpu.VMEM((rows, states), bf16),
             pltpu.VMEM((rows * chunks, LANES), f32),
             pltpu.VMEM((planes, rows, chunks, LANES), bf16),
-            pltpu.VMEM((planes, group, rows, sub, LANES), bf16),
+            pltpu.VMEM((planes, group, rows, per * sub, LANES), bf16),
             pltpu.VMEM((planes, 2, group // 2, rows, sub, LANES), bf16),
-            pltpu.VMEM((2, devices * (rows * sub + 1), LANES), f32),
+            pltpu.VMEM((3, devices * (rows * sub + 1), LANES), f32),
             pltpu.VMEM((2, width, width), bf16),
             pltpu.VMEM((2, rows * devices, width), bf16),
             pltpu.VMEM((rows * devices, width), f32),
+            pltpu.VMEM((rows, devices, LANES), f32),
             pltpu.VMEM((devices, 1, LANES), f32),
             pltpu.VMEM((devices, 1, LANES), f32),
             dma((3,)),
             dma((4 + planes,)),
             dma((planes, planes)),
-            dma((1,)),
+            dma((depth_count,)),
             dma((planes,)),
             dma((1,)),
             dma((planes,)),
@@ -509,7 +591,7 @@
     def shards(jacobian, gain_inverse, variance):
         width = gain_inverse.shape[1]
         fits = gain_inverse.size * gain_inverse.dtype.itemsize <= 16 * 1024 * 1024
-        paired = depth_count in (2, 4) and blk_count == 2 * depth_count
+        paired = 2 < depth_count <= 4 and depth_count % 2 == 0 and blk_count == 2 * depth_count
         if paired and width % (PACKED * LANES) == 0 and fits:
             return half_shards(jacobian, gain_inverse, variance)
         return plain_shards(jacobian, gain_inverse, variance)

time: 26.6 us -> 24.8 us (0.932)
  Pallas kernels: 25.3 us -> 24.2 us
  other arithmetic: 1.11 us -> 0.51 us
    pallas_call x1, Pallas kernels: 25.3 us -> 24.2 us  [half_shards(): pl.pallas_call(functools.partial(half_kernel, depth_count, blk_count, row...]
    sub x1, other arithmetic: 1.11 us -> 0.51 us  [half_shards(): return variance - quadratic[0, :rows]]
where the time goes in v4:
time: 24.8 us; the launch traced here: 24.7 us
  Pallas kernels  24.2 us (98%)
  other arithmetic  0.51 us (2%)
    pallas_call x1, Pallas kernels, half_shards(): pl.pallas_call(functools.partial(half_kernel, depth_count, blk_count, row...  24.2 us
    sub x1, other arithmetic, half_shards(): return variance - quadratic[0, :rows]  0.51 us

profile of v4, /device:TPU:0, one launch (start us, length us, event | category | flops | bytes accessed | tf_op | source)
XLA Modules:
  0.0 24.7 jit_solution(16412875853085153460)
XLA Ops:
  0.0 0.0 copy-start
  0.0 24.2 %shard_map.37 = f32[1,128]{1,0:T(1,128)S(1)} custom-call(bf16[3,16384]{1,0:T(4,128)(2,1)} %jac_ref.1, bf16[4096,2048]{1,0:T(8,128)(2,1)} %gain_ref.1), custom_call_target="tpu_custom_call" | custom-call | tf_op jit(solution)/shard_map/pallas_call | solution.py:549
  24.2 0.0 copy-done
  24.2 0.5 %bitcast_subtract_fusion = f32[3]{0:T(128)} fusion(f32[3]{0:T(128)S(1)} %copy-done, f32[1,128]{1,0:T(1,128)S(1)} %shard_map.37), kind=kLoop, calls=%fused_computation | loop fusion | flops 3 | bytes 36 | tf_op jit(solution)/shard_map/sub | solution.py:583
Async XLA Ops:
  0.0 24.2 %copy-start = (f32[3]{0:T(128)S(1)}, f32[3]{0:T(128)}, u32[]{:S(2)}) copy-start(f32[3]{0:T(128)} %param.5) | copy-start | bytes 40

commit v5 on v4

--- a/solution.py
+++ b/solution.py
@@ -148,14 +148,11 @@
     def at_end(z):
         return (z == 0) | (z == end)
 
-    def adjacent(d, z):
-        return (d - z == 1) | (z - d == 1)
-
     def takes_none(d, z):
-        return adjacent(d, z) & at_end(z)
+        return at_end(z) & jnp.logical_not(at_end(d))
 
     def takes_both(d, z):
-        return adjacent(d, z) & at_end(d)
+        return at_end(d) & jnp.logical_not(at_end(z))
 
     idle = takes_none(depth, plane)
     double = takes_both(depth, plane)
@@ -192,11 +189,11 @@
     jac_copy.start()
     gain_first = pltpu.make_async_copy(
         gain_ref.at[pl.ds(pl.multiple_of(jnp.where(double, 0, my_other - depth * per) * width, width), width), :],
-        gain.at[0], local_sem.at[1],
+        gain.at[pl.ds(0, width)], local_sem.at[1],
     )
     gain_second = pltpu.make_async_copy(
         gain_ref.at[pl.ds(pl.multiple_of(jnp.where(double, 1, side) * width, width), width), :],
-        gain.at[1], local_sem.at[2],
+        gain.at[pl.ds(width, width)], local_sem.at[2],
     )
 
     @pl.when(jnp.logical_not(idle))
@@ -242,16 +239,16 @@
         piece = lines.at[source, :, pl.ds(pl.multiple_of(part * (per * sub), per * sub), per * sub), :]
         return remote(piece, piece, send_sem, line_recv.at[source, part], depth, target * per + side)
 
-    def first_part(target):
-        return wrap(jnp.clip(target, 1, end - 1) + 1, planes)
+    def nth_part(target, k):
+        return jnp.where(2 * target < planes, wrap(planes - k, planes), wrap(end + k, planes))
 
     def part_count(target):
-        return jnp.where(at_end(target), planes - 1, planes)
-
-    def send_line(target, sem_at):
-        @pl.loop(0, part_count(target))
+        return jnp.where(at_end(target), 2, planes)
+
+    def send_line(target, sem_at, first, last):
+        @pl.loop(first, last)
         def _(k):
-            along(plane, wrap(first_part(target) + k, planes), target, line_send.at[sem_at]).start()
+            along(plane, nth_part(target, k), target, line_send.at[sem_at]).start()
 
     def seen_from(d, s):
         seen = spot - (d * per + s)
@@ -292,12 +289,6 @@
         )
 
     def spread(source, part):
-        @pl.when(part == plane)
-        def _():
-            for step in range(1, half_group):
-                to_panel(source, step).start()
-            own_to_twin(source).start()
-
         for s in range(per):
             foreign = (part != depth) | (side != s)
 
@@ -305,9 +296,14 @@
             def _():
                 to_both(source, part, s).start()
 
-            @pl.when(foreign & jnp.logical_not(adjacent(part, plane) & (at_end(part) | at_end(plane))))
+            @pl.when(foreign & (at_end(part) == at_end(plane)))
             def _():
                 to_other(source, part, s).start()
+
+    def spread_panel(source):
+        for step in range(1, half_group):
+            to_panel(source, step).start()
+        own_to_twin(source).start()
 
     def forward_panel(source):
         settle(panel_in.at[source, 0, pl.ds(1, half_group - 1)], panel_recv.at[source])
@@ -316,23 +312,31 @@
     for sem_at, known, away in ((1, two_down, -2), (3, plane > 0, -1), (2, plane < end, 1), (0, two_up, 2)):
         @pl.when(known)
         def _():
-            send_line(plane + away, sem_at)
+            send_line(plane + away, sem_at, 0, 2)
 
     @pl.loop(0, planes)
     def _(k):
-        spread(plane, wrap(plane + k, planes))
+        spread(plane, nth_part(plane, k))
+
+    spread_panel(plane)
 
     def relays(source):
         down = (plane == 1) & (source > 1)
         up = (plane == end - 1) & (source < end - 1)
         return down, up
 
+    def send_rest():
+        for sem_at, known, away in ((1, two_down, -2), (3, plane > 0, -1), (2, plane < end, 1), (0, two_up, 2)):
+            @pl.when(known & jnp.logical_not(at_end(plane + away)))
+            def _():
+                send_line(plane + away, sem_at, 2, planes)
+
     def receive(source, k):
         down, up = relays(source)
-        part = wrap(first_part(plane) + k, planes)
+        part = nth_part(plane, k)
         along(source, part, plane, line_send.at[0]).wait_recv()
 
-        @pl.when((down | up) & (k < planes - 1))
+        @pl.when((down | up) & (k < 2))
         def _():
             along(source, part, jnp.where(down, 0, end), line_send.at[4 + source]).start()
 
@@ -340,18 +344,34 @@
 
     @pl.when(at_end(plane))
     def _():
-        for source in sources:
-            @pl.loop(0, planes - 1)
+        for n, source in enumerate(sources):
+            @pl.loop(0, 2)
             def _(k):
                 receive(source, k)
+                if n == 0:
+                    @pl.when(k == 0)
+                    def _():
+                        send_rest()
+
+            if n:
+                spread_panel(sources[n - 1])
+
+        spread_panel(sources[-1])
 
     @pl.when(jnp.logical_not(at_end(plane)))
     def _():
-        for turn in (sources[:2], sources[2:]):
-            @pl.loop(0, planes)
-            def _(k):
-                for source in turn:
-                    receive(source, k)
+        receive(sources[0], 0)
+        send_rest()
+        receive(sources[1], 0)
+        for first, last in ((1, 2), (2, planes)):
+            for turn, start in ((sources[:2], first), (sources[2:], first - first % 2)):
+                @pl.loop(start, last)
+                def _(k):
+                    for source in turn:
+                        receive(source, k)
+
+        for source in sources:
+            spread_panel(source)
 
     def widen(index, slot, block):
         wide[index, pl.ds(slot * pitch, rows * sub), :] = block.reshape(rows * sub, LANES).astype(
@@ -400,70 +420,63 @@
     everything = [plane] + sources
     for source in everything:
         collect_other(source)
+
+    def columns(index, c):
+        return [wide[index, pl.ds(r * sub + c, devices, stride=pitch), :] for r in range(rows)]
+
+    def narrow(first, source):
+        for c in range(sub):
+            for r, block in enumerate(columns(source, c)):
+                left[r * devices : (r + 1) * devices, first + c * LANES : first + (c + 1) * LANES] = block.astype(
+                    jnp.bfloat16
+                )
+
+    def dot(first, count, n=slice(0, width)):
+        a = left[:, pl.ds(first, count)]
+        return jnp.dot(a, gain[pl.ds(first, count), n], preferred_element_type=jnp.float32)
+
+    half = width // 2
+    halves = [slice(0, half), slice(half, width)]
+
+    @pl.when(jnp.logical_not(idle))
+    def _():
+        narrow(0, 0)
+        gain_first.wait()
+
+    @pl.when(double)
+    def _():
+        narrow(width, 2)
+        gain_second.wait()
+
+    def multiply(n):
+        at = halves[n]
+
+        @pl.when(single & jnp.logical_not(on_diagonal))
+        def _():
+            projected[:, at] = dot(0, width, at)
+
+        @pl.when(double)
+        def _():
+            projected[:, at] = dot(0, 2 * width, at)
+
+        @pl.when(on_diagonal)
+        def _():
+            quarter = pl.multiple_of(jnp.where(side == 0, n, 1 - n) * half, half)
+            projected[:, at] = dot(quarter, half, at)
+
+    multiply(0)
     for source in everything:
         forward_panel(source)
-
-    def columns(index, c):
-        return [wide[index, pl.ds(r * sub + c, devices, stride=pitch), :] for r in range(rows)]
-
-    def narrow(index, source):
-        for c in range(sub):
-            for r, block in enumerate(columns(source, c)):
-                left[index, r * devices : (r + 1) * devices, c * LANES : (c + 1) * LANES] = block.astype(
-                    jnp.bfloat16
-                )
-
-    block_width = width // 4
-    blocks = width // block_width
-    inner = block_width // LANES
-
-    def dot(index, first, count, n):
-        if isinstance(first, int):
-            a = left[index, :, first : first + count]
-        else:
-            a = left[index, :, pl.ds(pl.multiple_of(first, LANES), count)]
-        b = gain[index, pl.ds(first, count), n * block_width : (n + 1) * block_width]
-        return jnp.dot(a, b, preferred_element_type=jnp.float32)
-
-    def columns_of(n):
-        return slice(n * block_width, (n + 1) * block_width)
-
-    @pl.when(jnp.logical_not(idle))
-    def _():
-        narrow(0, 0)
-        gain_first.wait()
-
-    @pl.when(single & jnp.logical_not(on_diagonal))
-    def _():
-        for n in range(blocks):
-            projected[:, columns_of(n)] = dot(0, 0, width, n)
-
-    @pl.when(double)
-    def _():
-        narrow(1, 2)
-        gain_second.wait()
-        for n in range(blocks):
-            projected[:, columns_of(n)] = dot(0, 0, width, n) + dot(1, 0, width, n)
-
-    @pl.when(on_diagonal)
-    def _():
-        for n in range(blocks):
-            later = 1 if 2 * n >= blocks else 0
-            quarter = jnp.where(side == 0, later, 1 - later) * (width // 2)
-            projected[:, columns_of(n)] = dot(0, quarter, width // 2, n)
-
+    multiply(1)
     for source in everything:
         collect_panel(source)
 
     @pl.when(on_diagonal)
     def _():
-        narrow(1, 1)
+        narrow(width, 1)
         gain_second.wait()
-        for n in range(blocks):
-            at = columns_of(n)
-            if n:
-                projected[:, at] += dot(1, 0, n * block_width, n)
-            projected[:, at] += dot(1, n * block_width, block_width, n) * 0.5
+        projected[:, halves[0]] += 0.5 * dot(width, half, halves[0])
+        projected[:, halves[1]] += dot(width, half, halves[1]) + 0.5 * dot(width + half, half, halves[1])
 
     @pl.when(idle)
     def _():
@@ -502,7 +515,7 @@
     def line_left(cond, target, sem):
         @pl.when(cond & at_end(target))
         def _():
-            settle(lines.at[0, :, pl.ds(0, (planes - 1) * per * sub)], sem)
+            settle(lines.at[0, :, pl.ds(0, 2 * per * sub)], sem)
 
         @pl.when(cond & jnp.logical_not(at_end(target)))
         def _():
@@ -558,8 +571,8 @@
             pltpu.VMEM((planes, group, rows, per * sub, LANES), bf16),
             pltpu.VMEM((planes, 2, group // 2, rows, sub, LANES), bf16),
             pltpu.VMEM((3, devices * (rows * sub + 1), LANES), f32),
-            pltpu.VMEM((2, width, width), bf16),
-            pltpu.VMEM((2, rows * devices, width), bf16),
+            pltpu.VMEM((2 * width, width), bf16),
+            pltpu.VMEM((rows * devices, 2 * width), bf16),
             pltpu.VMEM((rows * devices, width), f32),
             pltpu.VMEM((rows, devices, LANES), f32),
             pltpu.VMEM((devices, 1, LANES), f32),

time: 24.8 us -> 23.6 us (0.952)
  Pallas kernels: 24.2 us -> 22.9 us
    pallas_call x1, Pallas kernels: 24.2 us -> 22.9 us  [half_shards(): pl.pallas_call(functools.partial(half_kernel, depth_count, blk_count, row...]
where the time goes in v5:
time: 23.6 us; the launch traced here: 23.5 us
  Pallas kernels  22.9 us (97%)
  other arithmetic  0.51 us (2%)
    pallas_call x1, Pallas kernels, half_shards(): pl.pallas_call(functools.partial(half_kernel, depth_count, blk_count, row...  22.9 us
    sub x1, other arithmetic, half_shards(): return variance - quadratic[0, :rows]  0.51 us

profile of v5, /device:TPU:0, one launch (start us, length us, event | category | flops | bytes accessed | tf_op | source)
XLA Modules:
  0.0 23.5 jit_solution(2457318617531238752)
XLA Ops:
  0.0 0.0 copy-start
  0.0 22.9 %shard_map.37 = f32[1,128]{1,0:T(1,128)S(1)} custom-call(bf16[3,16384]{1,0:T(4,128)(2,1)} %jac_ref.1, bf16[4096,2048]{1,0:T(8,128)(2,1)} %gain_ref.1), custom_call_target="tpu_custom_call" | custom-call | tf_op jit(solution)/shard_map/pallas_call | solution.py:562
  23.0 0.0 copy-done
  23.0 0.5 %bitcast_subtract_fusion = f32[3]{0:T(128)} fusion(f32[3]{0:T(128)S(1)} %copy-done, f32[1,128]{1,0:T(1,128)S(1)} %shard_map.37), kind=kLoop, calls=%fused_computation | loop fusion | flops 3 | bytes 36 | tf_op jit(solution)/shard_map/sub | solution.py:596
Async XLA Ops:
  0.0 23.0 %copy-start = (f32[3]{0:T(128)S(1)}, f32[3]{0:T(128)}, u32[]{:S(2)}) copy-start(f32[3]{0:T(128)} %param.5) | copy-start | bytes 40

commit v6 on v5

--- a/solution.py
+++ b/solution.py
@@ -122,7 +122,7 @@
     depth_count, blk_count, rows, jac_ref, gain_ref, out_ref,
     own_raw, own_wide, lines, other_in, panel_in, wide, gain, left, projected, partial, outgoing, arrived,
     local_sem, line_send, line_recv, other_send, other_recv,
-    panel_send, panel_recv, twin_send, twin_recv, last_send, last_recv,
+    panel_send, panel_recv, twin_send, twin_recv, last_send, last_recv, far_sem,
 ):
     per = blk_count // depth_count
     planes = depth_count
@@ -165,6 +165,9 @@
     two_up = inside(plane + 2)
     two_down = inside(plane - 2)
 
+    def near(d, s):
+        return (d // 2 == depth // 2) | (s == side)
+
     def wrap(value, count):
         return jnp.where(value >= count, value - count, value)
 
@@ -211,7 +214,10 @@
 
     for s in range(1, group):
         member = wrap(spot + s, group)
-        greet(member // per, plane * per + lax.rem(member, per))
+
+        @pl.when(near(member // per, lax.rem(member, per)))
+        def _():
+            greet(member // per, plane * per + lax.rem(member, per))
 
     for away in (1, -1, 2, -2):
         known = (plane + away >= 0) & (plane + away <= end)
@@ -230,10 +236,14 @@
     for r in range(rows):
         lines[plane, r] = own_wide[r * chunks : (r + 1) * chunks, :].astype(jnp.bfloat16)
 
-    heard = group - 1
+    heard = 2 * per - 1 + depth_count - 2
     for known in (plane > 0, plane < end, two_up, two_down):
         heard = heard + jnp.where(known, 1, 0)
     pl.semaphore_wait(barrier, heard)
+
+    pl.semaphore_signal(
+        far_sem, inc=1, device_id={"depth": depth, "blk": plane * per + per - 1 - side}, device_id_type=MESH
+    )
 
     def along(source, part, target, send_sem):
         piece = lines.at[source, :, pl.ds(pl.multiple_of(part * (per * sub), per * sub), per * sub), :]
@@ -288,9 +298,11 @@
             twin_send.at[0], twin_recv.at[source], twin, blk,
         )
 
-    def spread(source, part):
+    def spread(source, part, which=None):
         for s in range(per):
             foreign = (part != depth) | (side != s)
+            if which is not None:
+                foreign = foreign & (near(part, s) == which)
 
             @pl.when(foreign & takes_both(part, plane))
             def _():
@@ -316,7 +328,13 @@
 
     @pl.loop(0, planes)
     def _(k):
-        spread(plane, nth_part(plane, k))
+        spread(plane, nth_part(plane, k), True)
+
+    pl.semaphore_wait(far_sem, 1)
+
+    @pl.loop(0, planes)
+    def _(k):
+        spread(plane, nth_part(plane, k), False)
 
     spread_panel(plane)
 
@@ -362,13 +380,13 @@
     def _():
         receive(sources[0], 0)
         send_rest()
-        receive(sources[1], 0)
-        for first, last in ((1, 2), (2, planes)):
-            for turn, start in ((sources[:2], first), (sources[2:], first - first % 2)):
-                @pl.loop(start, last)
-                def _(k):
-                    for source in turn:
-                        receive(source, k)
+        for source, first, stop in (
+            (sources[0], 1, 2), (sources[1], 0, 2), (sources[2], 0, 2),
+            (sources[0], 2, planes), (sources[1], 2, planes), (sources[2], 2, planes),
+        ):
+            @pl.loop(first, stop)
+            def _(k):
+                receive(source, k)
 
         for source in sources:
             spread_panel(source)
@@ -588,6 +606,7 @@
             dma((planes,)),
             dma((1,)),
             dma((1,)),
+            pltpu.SemaphoreType.REGULAR,
         ],
         compiler_params=pltpu.CompilerParams(
             collective_id=0, has_side_effects=True, vmem_limit_bytes=60 * 1024 * 1024

time: 23.6 us -> 23.1 us (0.979)
  Pallas kernels: 22.9 us -> 22.4 us
    pallas_call x1, Pallas kernels: 22.9 us -> 22.4 us  [half_shards(): pl.pallas_call(functools.partial(half_kernel, depth_count, blk_count, row...]
where the time goes in v6:
time: 23.1 us; the launch traced here: 22.9 us
  Pallas kernels  22.4 us (97%)
  other arithmetic  0.51 us (2%)
    pallas_call x1, Pallas kernels, half_shards(): pl.pallas_call(functools.partial(half_kernel, depth_count, blk_count, row...  22.4 us
    sub x1, other arithmetic, half_shards(): return variance - quadratic[0, :rows]  0.51 us

profile of v6, /device:TPU:0, one launch (start us, length us, event | category | flops | bytes accessed | tf_op | source)
XLA Modules:
  0.0 22.9 jit_solution(3552495299071053896)
XLA Ops:
  0.0 0.0 copy-start
  0.0 22.4 %shard_map.37 = f32[1,128]{1,0:T(1,128)S(1)} custom-call(bf16[3,16384]{1,0:T(4,128)(2,1)} %jac_ref.1, bf16[4096,2048]{1,0:T(8,128)(2,1)} %gain_ref.1), custom_call_target="tpu_custom_call" | custom-call | tf_op jit(solution)/shard_map/pallas_call | solution.py:580
  22.4 0.0 copy-done
  22.4 0.5 %bitcast_subtract_fusion = f32[3]{0:T(128)} fusion(f32[3]{0:T(128)S(1)} %copy-done, f32[1,128]{1,0:T(1,128)S(1)} %shard_map.37), kind=kLoop, calls=%fused_computation | loop fusion | flops 3 | bytes 36 | tf_op jit(solution)/shard_map/sub | solution.py:615
Async XLA Ops:
  0.0 22.4 %copy-start = (f32[3]{0:T(128)S(1)}, f32[3]{0:T(128)}, u32[]{:S(2)}) copy-start(f32[3]{0:T(128)} %param.5) | copy-start | bytes 40
